TPU v7x, 32 devices: a whole 2x2x4 slice. The times are simulated.
32 devices in a mesh: prow: 4 (over y, core), pcol: 8 (over z, x).
Axes of the slice: x: 2, y: 2, z: 4, core: 2. Of those that a mesh axis runs over, the one named last changes fastest.
Arguments:
- matrix: bfloat16 [2, 8, 4, 256, 2, 8, 256], P(None, None, 'prow', None, None, 'pcol'), may hold values from -6 to 6
Outputs:
- image: float32 [2, 8, 4, 256, 2, 8, 256], P(None, None, 'prow', None, None, 'pcol')
All inputs are finite; a program needn't handle non-finite values.
Results may differ from a plain program's by a relative error of at most 0.0003.
Values sent between devices are 32-bit elements; how exact they have to be, the bound alone decides.
A program may use at most 64 MiB of HBM per device.

v0:
```python
import jax
import jax.numpy as jnp
from jax import lax
from jax.sharding import PartitionSpec as P

HIGH = lax.Precision.HIGHEST


def prefix(value, axis, combine, identity):
    length, here = (lax.axis_size(axis), lax.axis_index(axis))
    everything = lax.all_gather(value, axis)
    start = jnp.broadcast_to(jnp.asarray(identity, value.dtype), value.shape)

    def lap(k, before):
        reached = k < here
        new = combine(before, everything[k])
        return jnp.where(reached, new, before)

    return lax.fori_loop(0, length, lap, start)


def add_terms(earlier, later):
    return earlier + later


def shards(matrix):
    batch = matrix.shape[0]
    rows_here = matrix.shape[1]
    tile_len = matrix.shape[3]
    cols_here = matrix.shape[4]
    prow_count = lax.axis_size("prow")
    pcol_count = lax.axis_size("pcol")
    prow_index = lax.axis_index("prow")
    pcol_index = lax.axis_index("pcol")
    local = matrix.astype(jnp.float32).reshape(batch, rows_here, tile_len, cols_here, tile_len)
    first_idx = lax.broadcasted_iota(jnp.int32, (tile_len, tile_len), 0)
    second_idx = lax.broadcasted_iota(jnp.int32, (tile_len, tile_len), 1)
    upper = (first_idx <= second_idx).astype(jnp.float32)
    lower = (second_idx <= first_idx).astype(jnp.float32)
    rowscan = jnp.einsum("nrick,kj->nricj", local, upper, precision=HIGH)
    row_sums = rowscan[:, :, :, :, tile_len - 1]
    gathered = lax.all_gather(row_sums, "pcol", axis=3, tiled=True)
    source = jnp.arange(pcol_count * cols_here, dtype=jnp.int32)
    source_glob = source % cols_here * pcol_count + source // cols_here
    target_glob = jnp.arange(cols_here, dtype=jnp.int32) * pcol_count + pcol_index
    earlier_mask = (source_glob[:, None] < target_glob[None, :]).astype(jnp.float32)
    row_carry = jnp.einsum("nrig,gc->nric", gathered, earlier_mask, precision=HIGH)
    rowscan = rowscan + row_carry[:, :, :, :, None]
    colscan = jnp.einsum("ik,nrkcj->nricj", lower, rowscan, precision=HIGH)
    col_sums = colscan[:, :, tile_len - 1, :, :]
    before = prefix(col_sums, "prow", add_terms, jnp.zeros_like(col_sums))
    whole = lax.psum(col_sums, "prow")
    strict = (jnp.arange(rows_here)[:, None] < jnp.arange(rows_here)[None, :]).astype(jnp.float32)
    col_carry = before + jnp.einsum("nscj,sr->nrcj", whole, strict, precision=HIGH)
    colscan = colscan + col_carry[:, :, None, :, :]
    row_glob = (
        jnp.arange(rows_here, dtype=jnp.int32)[:, None] * prow_count + prow_index
    ) * tile_len + jnp.arange(tile_len, dtype=jnp.int32)[None, :]
    col_glob = (
        jnp.arange(cols_here, dtype=jnp.int32)[:, None] * pcol_count + pcol_index
    ) * tile_len + jnp.arange(tile_len, dtype=jnp.int32)[None, :]
    row_factor = 1.0 / jnp.sqrt(row_glob.astype(jnp.float32) + 1.0)
    col_factor = 1.0 / jnp.sqrt(col_glob.astype(jnp.float32) + 1.0)
    scaled = colscan * (row_factor[None, :, :, None, None] * col_factor[None, None, None, :, :])
    return scaled.reshape(batch, rows_here, 1, tile_len, cols_here, 1, tile_len)


def solution(mesh):
    return jax.shard_map(
        shards,
        mesh=mesh,
        in_specs=(P(None, None, "prow", None, None, "pcol", None),),
        out_specs=P(None, None, "prow", None, None, "pcol", None),
        check_vma=False,
    )
```

profile of v0, /device:TPU:0, one launch (start us, length us, event | category | flops | bytes accessed | tf_op | source)
XLA Modules:
  0.0 76.3 jit_solution(13902189001919219110)
XLA Ops:
  0.0 3.5 %fusion.8 = f32[2,8,256,2,256]{2,4,3,1,0:T(8,128)S(1)} fusion(bf16[2,8,256,2,256]{4,3,2,1,0:T(2,128)(2,1)} %bitcast.44), kind=kOutput, calls=%fused_computation.10 | convolution fusion | flops 1073807360 | bytes 12582912 | tf_op jit(solution)/shard_map/nrick,kj->nricj/dot_general | solution.py:40
  3.5 28.3 %all-gather = f32[2,8,256,16,1]{2,4,3,1,0:T(1,128)S(1)} all-gather(f32[2,8,256,2,1]{2,4,3,1,0:T(1,128)S(1)} %slice.8), channel_id=2, replica_groups=mesh['prow'=4,'pcol'=8] {'pcol'}, dimensions={3}, use_global_device_ids=true | all-gather | bytes 294912 | tf_op jit(solution)/shard_map/all_gather | solution.py:42
  31.9 0.3 fusion.12
  32.2 4.9 %fusion.5 = f32[2,8,256,2,256]{4,2,3,1,0:T(8,128)S(1)} fusion(f32[2,8,256,2,256]{2,4,3,1,0:T(8,128)S(1)} %fusion.8, f32[2,8,256,2]{2,3,1,0:T(2,128)S(1)} %fusion.12), kind=kOutput, calls=%fused_computation.9 | convolution fusion | flops 6444613632 | bytes 16809984 | tf_op jit(solution)/shard_map/ik,nrkcj->nricj/dot_general | solution.py:49
  37.2 0.0 copy-start
  37.2 3.4 %copy-done = f32[2,8,256,2,256]{4,2,3,1,0:T(8,128)} copy-done((f32[2,8,256,2,256]{4,2,3,1,0:T(8,128)}, f32[2,8,256,2,256]{4,2,3,1,0:T(8,128)S(1)}, u32[]{:S(2)}) %copy-start) | copy-done | bytes 8388632
  40.6 5.4 %all-gather.1 = f32[8,8,1,2,256]{4,1,3,2,0:T(8,128)S(1)} all-gather(f32[2,8,1,2,256]{4,1,3,2,0:T(8,128)S(1)} %copy.10), channel_id=3, replica_groups=mesh['prow'=4,'pcol'=8] {'prow'}, dimensions={0}, use_global_device_ids=true | all-gather | bytes 163840 | tf_op jit(solution)/shard_map/all_gather | solution.py:11
  46.0 0.3 while.14
  46.3 11.6 %psum.7 = f32[2,8,2,256]{3,2,1,0:T(2,128)S(1)} all-reduce(f32[2,8,2,256]{3,2,1,0:T(2,128)S(1)} %bitcast.46), channel_id=1, replica_groups=mesh['prow'=4,'pcol'=8] {'prow'}, use_global_device_ids=true, to_apply=%region_2.3 | all-reduce | flops 8192 | bytes 65536 | tf_op jit(solution)/shard_map/psum | solution.py:52
  58.0 0.1 fusion.11
  58.1 0.1 add_rsqrt_fusion
  58.2 0.1 add_rsqrt_fusion.1
  58.3 2.3 %broadcast_multiply_fusion = f32[8,256,2,256]{3,1,2,0:T(8,128)} fusion(f32[2,256]{1,0:T(2,128)S(1)} %add_rsqrt_fusion.1, f32[8,256]{1,0:T(8,128)S(1)} %add_rsqrt_fusion), kind=kLoop, calls=%fused_computation.11 | loop fusion | flops 1048576 | bytes 4204544 | tf_op jit(solution)/shard_map/mul | solution.py:64
  60.6 5.8 %multiply_bitcast_fusion = f32[2,8,1,256,2,1,256]{6,3,4,1,0,5,2:T(8,128)S(1)} fusion(f32[2,8,256,2,256]{4,2,3,1,0:T(8,128)} %copy-done, f32[8,256,2,256]{3,1,2,0:T(8,128)} %broadcast_multiply_fusion, f32[2,8,2,256]{3,2,1,0:T(2,128)S(1)} %copy.14), kind=kLoop, calls=%fused_computation.3 | loop fusion | flops 4194304 | bytes 21004288 | tf_op jit(solution)/shard_map/reshape | solution.py:65
  66.4 9.9 %copy.15 = f32[2,8,1,256,2,1,256]{6,5,4,3,2,1,0:T(1,128)} copy(f32[2,8,1,256,2,1,256]{6,3,4,1,0,5,2:T(8,128)S(1)} %multiply_bitcast_fusion) | data formatting | bytes 16777216 | tf_op jit(solution)/shard_map/reshape | solution.py:65
  (18 shorter events, 0.3 us)
Async XLA Ops:
  37.2 3.4 %copy-start = (f32[2,8,256,2,256]{4,2,3,1,0:T(8,128)}, f32[2,8,256,2,256]{4,2,3,1,0:T(8,128)S(1)}, u32[]{:S(2)}) copy-start(f32[2,8,256,2,256]{4,2,3,1,0:T(8,128)S(1)} %fusion.5) | copy-start | bytes 25165828
where the time goes:
time: 76.5 us; the launch traced here: 76.3 us
  blocking collectives  45.4 us (59%)
  local copies, waits for them, and re-layouts  13.4 us (18%)
  matrix products  8.87 us (12%)
  other arithmetic  8.4 us (11%)
    all_gather x1, blocking collectives, shards(): gathered = lax.all_gather(row_sums, 'pcol', axis=3, tiled=True)  28.3 us
    psum x1, blocking collectives, shards(): whole = lax.psum(col_sums, 'prow')  11.6 us
    reshape x1, local copies, waits for them, and re-layouts, shards(): return scaled.reshape(batch, rows_here, 1, tile_len, cols_here, 1, tile_len)  9.91 us
    reshape x1, other arithmetic, shards(): return scaled.reshape(batch, rows_here, 1, tile_len, cols_here, 1, tile_len)  5.81 us
    all_gather x1, blocking collectives, prefix(): everything = lax.all_gather(value, axis)  5.42 us
    dot_general x1, matrix products, shards(): colscan = jnp.einsum('ik,nrkcj->nricj', lower, rowscan, precision=HIGH)  4.93 us
    dot_general x1, matrix products, shards(): rowscan = jnp.einsum('nrick,kj->nricj', local, upper, precision=HIGH)  3.48 us
    unnamed x3, local copies, waits for them, and re-layouts  3.41 us

commit v1 on v0

--- a/solution.py
+++ b/solution.py
@@ -39,12 +39,41 @@
     lower = (second_idx <= first_idx).astype(jnp.float32)
     rowscan = jnp.einsum("nrick,kj->nricj", local, upper, precision=HIGH)
     row_sums = rowscan[:, :, :, :, tile_len - 1]
-    gathered = lax.all_gather(row_sums, "pcol", axis=3, tiled=True)
     source = jnp.arange(pcol_count * cols_here, dtype=jnp.int32)
     source_glob = source % cols_here * pcol_count + source // cols_here
     target_glob = jnp.arange(cols_here, dtype=jnp.int32) * pcol_count + pcol_index
     earlier_mask = (source_glob[:, None] < target_glob[None, :]).astype(jnp.float32)
-    row_carry = jnp.einsum("nrig,gc->nric", gathered, earlier_mask, precision=HIGH)
+    size, index, width = (lax.axis_size("pcol"), lax.axis_index("pcol"), row_sums.shape[3])
+    forward = [(i, (i + 1) % size) for i in range(size)]
+    behind = [(i, (i - 1) % size) for i in range(size)]
+    middle = size // 2
+    from_left = from_right = row_sums
+    row_carry = jnp.einsum(
+        "nrig,gc->nric",
+        row_sums,
+        lax.dynamic_slice_in_dim(earlier_mask, index * width, row_sums.shape[3], axis=0),
+        precision=HIGH,
+    )
+    for step in range(1, middle + 1):
+        from_left = lax.ppermute(from_left, "pcol", forward)
+        if step < size - middle:
+            from_right = lax.ppermute(from_right, "pcol", behind)
+            row_carry = row_carry + jnp.einsum(
+                "nrig,gc->nric",
+                from_right,
+                lax.dynamic_slice_in_dim(
+                    earlier_mask, (index + step) % size * width, from_right.shape[3], axis=0
+                ),
+                precision=HIGH,
+            )
+        row_carry = row_carry + jnp.einsum(
+            "nrig,gc->nric",
+            from_left,
+            lax.dynamic_slice_in_dim(
+                earlier_mask, (index - step) % size * width, from_left.shape[3], axis=0
+            ),
+            precision=HIGH,
+        )
     rowscan = rowscan + row_carry[:, :, :, :, None]
     colscan = jnp.einsum("ik,nrkcj->nricj", lower, rowscan, precision=HIGH)
     col_sums = colscan[:, :, tile_len - 1, :, :]

time: 76.5 us -> 83.9 us (1.097)
  blocking collectives: 45.4 us -> 17 us
  starting transfers between devices: 0 us -> 15.6 us
  waiting for transfers between devices: 0 us -> 12.3 us
  matrix products: 8.87 us -> 13 us
  local copies, waits for them, and re-layouts: 13.4 us -> 16.8 us
    all_gather x1 -> x0, blocking collectives: 28.3 us -> none  [shards(): gathered = lax.all_gather(row_sums, 'pcol', axis=3, tiled=True)]
    ppermute x0 -> x7, starting transfers between devices: none -> 15.6 us  [the longest x3 15.5 us: shards(): from_right = lax.ppermute(from_right, 'pcol', behind)]
    ppermute x0 -> x7, waiting for transfers between devices: none -> 12.3 us  [the longest x4 12.3 us: shards(): from_left = lax.ppermute(from_left, 'pcol', forward)]
    unnamed x3 -> x6, local copies, waits for them, and re-layouts: 3.41 us -> 6.82 us
    dot_general x1, matrix products: 4.93 us -> 7.27 us  [shards(): colscan = jnp.einsum('ik,nrkcj->nricj', lower, rowscan, precision=HIGH)]
    dot_general x1 -> x8, matrix products: 0.32 us -> 2.09 us  [the longest x4 1.04 us: shards(): jnp.einsum('nrig,gc->nric', from_left, lax.dynamic_slice_in_dim(earlier_m...]
  transfers between devices with their start and end apart: 0 -> 7, of which waited for: 0 -> 4; matrix products, arithmetic and copies ran while one was open for 0% -> 5% of each run, Pallas kernels for 0% -> 0%
where the time goes in v1:
time: 83.9 us; the launch traced here: 83.7 us
  blocking collectives  17 us (20%)
  local copies, waits for them, and re-layouts  16.8 us (20%)
  starting transfers between devices  15.6 us (19%)
  matrix products  13 us (15%)
  waiting for transfers between devices  12.3 us (15%)
  other arithmetic  8.5 us (10%)
    ppermute x3, starting transfers between devices, shards(): from_right = lax.ppermute(from_right, 'pcol', behind)  15.5 us
    ppermute x4, waiting for transfers between devices, shards(): from_left = lax.ppermute(from_left, 'pcol', forward)  12.3 us
    psum x1, blocking collectives, shards(): whole = lax.psum(col_sums, 'prow')  11.6 us
    reshape x1, local copies, waits for them, and re-layouts, shards(): return scaled.reshape(batch, rows_here, 1, tile_len, cols_here, 1, tile_len)  9.91 us
    dot_general x1, matrix products, shards(): colscan = jnp.einsum('ik,nrkcj->nricj', lower, rowscan, precision=HIGH)  7.27 us
    unnamed x6, local copies, waits for them, and re-layouts  6.82 us
    reshape x1, other arithmetic, shards(): return scaled.reshape(batch, rows_here, 1, tile_len, cols_here, 1, tile_len)  5.82 us
    all_gather x1, blocking collectives, prefix(): everything = lax.all_gather(value, axis)  5.42 us
  transfers between devices with their start and end apart: 7, of which 4 were waited for; matrix products, arithmetic and copies ran while one was open for 5% of the time, Pallas kernels for 0%

profile of v1, /device:TPU:0, one launch (start us, length us, event | category | flops | bytes accessed | tf_op | source)
XLA Modules:
  0.0 83.7 jit_solution(17544186583274987937)
XLA Ops:
  0.0 3.5 %fusion.8 = f32[2,8,256,2,256]{2,4,3,1,0:T(8,128)S(1)} fusion(bf16[2,8,256,2,256]{4,3,2,1,0:T(2,128)(2,1)} %bitcast.87), kind=kOutput, calls=%fused_computation.10 | convolution fusion | flops 1073807360 | bytes 12582912 | tf_op jit(solution)/shard_map/nrick,kj->nricj/dot_general | solution.py:40
  3.5 0.0 copy-start.1
  3.5 3.4 %copy-done.1 = f32[2,8,256,2,256]{2,4,3,1,0:T(8,128)} copy-done((f32[2,8,256,2,256]{2,4,3,1,0:T(8,128)}, f32[2,8,256,2,256]{2,4,3,1,0:T(8,128)S(1)}, u32[]{:S(2)}) %copy-start.1) | copy-done | bytes 8388632
  6.9 6.1 %collective-permute-start = (f32[2,8,256,2]{2,3,1,0:T(2,128)S(1)}, f32[2,8,256,2]{2,3,1,0:T(2,128)S(1)}, u32[]{:S(2)}, u32[]{:S(2)}) collective-permute-start(f32[2,8,256,2]{2,3,1,0:T(2,128)S(1)} %bitcast.89), channel_id=1, source_target_pairs={{0,7},{1,0},{2,1},{3,2},{4,3},{5,4},{6,5},{7,6},{8,15},{9,8},{10,9... | collective-permute-start | bytes 98312 | tf_op jit(solution)/shard_map/ppermute | solution.py:60
  13.0 0.0 collective-permute-start.1
  13.0 0.1 add_rsqrt_fusion.1
  13.1 0.1 add_rsqrt_fusion
  13.2 0.1 broadcast_compare_fusion
  13.3 2.3 %broadcast_multiply_fusion = f32[8,256,2,256]{3,1,2,0:T(8,128)} fusion(f32[2,256]{1,0:T(2,128)S(1)} %add_rsqrt_fusion.1, f32[8,256]{1,0:T(8,128)S(1)} %add_rsqrt_fusion), kind=kLoop, calls=%fused_computation.11 | loop fusion | flops 1048576 | bytes 4204544 | tf_op jit(solution)/shard_map/mul | solution.py:93
  15.6 0.3 fusion.22
  16.0 3.6 %collective-permute-done.1 = f32[2,8,256,2]{2,3,1,0:T(2,128)S(1)} collective-permute-done((f32[2,8,256,2]{2,3,1,0:T(2,128)S(1)}, f32[2,8,256,2]{2,3,1,0:T(2,128)S(1)}, u32[]{:S(2)}, u32[]{:S(2)}) %collective-permute-start.1) | collective-permute-done | bytes 32800 | tf_op jit(solution)/shard_map/ppermute | solution.py:58
  19.6 0.0 collective-permute-start.3
  19.6 0.0 collective-permute-done
  19.6 4.7 %collective-permute-start.2 = (f32[2,8,256,2]{2,3,1,0:T(2,128)S(1)}, f32[2,8,256,2]{2,3,1,0:T(2,128)S(1)}, u32[]{:S(2)}, u32[]{:S(2)}) collective-permute-start(f32[2,8,256,2]{2,3,1,0:T(2,128)S(1)} %collective-permute-done), channel_id=1, source_target_pairs={{0,7},{1,0},{2,1},{3,2},{4,3},{5,4},{6,5},{7,6},{8,15},{9,8},{10,9... | collective-permute-start | bytes 98312 | tf_op jit(solution)/shard_map/ppermute | solution.py:60
  24.3 0.3 convolution_add_fusion.4
  24.6 0.3 convolution_add_fusion.3
  24.9 1.3 %collective-permute-done.3 = f32[2,8,256,2]{2,3,1,0:T(2,128)S(1)} collective-permute-done((f32[2,8,256,2]{2,3,1,0:T(2,128)S(1)}, f32[2,8,256,2]{2,3,1,0:T(2,128)S(1)}, u32[]{:S(2)}, u32[]{:S(2)}) %collective-permute-start.3) | collective-permute-done | bytes 32800 | tf_op jit(solution)/shard_map/ppermute | solution.py:58
  26.2 0.0 collective-permute-start.5
  26.2 0.3 fusion.31
  26.5 0.0 collective-permute-done.2
  26.5 4.8 %collective-permute-start.4 = (f32[2,8,256,2]{2,3,1,0:T(2,128)S(1)}, f32[2,8,256,2]{2,3,1,0:T(2,128)S(1)}, u32[]{:S(2)}, u32[]{:S(2)}) collective-permute-start(f32[2,8,256,2]{2,3,1,0:T(2,128)S(1)} %collective-permute-done.2), channel_id=1, source_target_pairs={{0,7},{1,0},{2,1},{3,2},{4,3},{5,4},{6,5},{7,6},{8,15},{9,8},{10,9... | collective-permute-start | bytes 98312 | tf_op jit(solution)/shard_map/ppermute | solution.py:60
  31.3 0.3 fusion.13
  31.6 1.3 %collective-permute-done.5 = f32[2,8,256,2]{2,3,1,0:T(2,128)S(1)} collective-permute-done((f32[2,8,256,2]{2,3,1,0:T(2,128)S(1)}, f32[2,8,256,2]{2,3,1,0:T(2,128)S(1)}, u32[]{:S(2)}, u32[]{:S(2)}) %collective-permute-start.5) | collective-permute-done | bytes 32800 | tf_op jit(solution)/shard_map/ppermute | solution.py:58
  32.8 0.0 collective-permute-start.6
  32.8 0.3 fusion.36
  33.1 0.0 collective-permute-done.4
  33.1 0.3 fusion.12
  33.4 6.1 %collective-permute-done.6 = f32[2,8,256,2]{2,3,1,0:T(2,128)S(1)} collective-permute-done((f32[2,8,256,2]{2,3,1,0:T(2,128)S(1)}, f32[2,8,256,2]{2,3,1,0:T(2,128)S(1)}, u32[]{:S(2)}, u32[]{:S(2)}) %collective-permute-start.6) | collective-permute-done | bytes 32800 | tf_op jit(solution)/shard_map/ppermute | solution.py:58
  39.5 0.3 convolution_add_fusion
  39.7 7.3 %fusion.5 = f32[2,8,256,2,256]{4,2,3,1,0:T(8,128)S(1)} fusion(f32[2,8,256,2,256]{2,4,3,1,0:T(8,128)} %copy-done.1, f32[2,8,256,2]{2,3,1,0:T(2,128)S(1)} %convolution_add_fusion), kind=kOutput, calls=%fused_computation.9 | convolution fusion | flops 6444613632 | bytes 16809984 | tf_op jit(solution)/shard_map/ik,nrkcj->nricj/dot_general | solution.py:78
  47.0 0.0 copy-start
  47.0 3.4 %copy-done = f32[2,8,256,2,256]{4,2,3,1,0:T(8,128)} copy-done((f32[2,8,256,2,256]{4,2,3,1,0:T(8,128)}, f32[2,8,256,2,256]{4,2,3,1,0:T(8,128)S(1)}, u32[]{:S(2)}) %copy-start) | copy-done | bytes 8388632
  50.5 5.4 %all-gather = f32[8,8,1,2,256]{4,1,3,2,0:T(8,128)S(1)} all-gather(f32[2,8,1,2,256]{4,1,3,2,0:T(8,128)S(1)} %copy.10), channel_id=2, replica_groups=mesh['prow'=4,'pcol'=8] {'prow'}, dimensions={0}, use_global_device_ids=true | all-gather | bytes 163840 | tf_op jit(solution)/shard_map/all_gather | solution.py:11
  55.9 0.3 while.14
  56.2 11.6 %psum.7 = f32[2,8,2,256]{3,2,1,0:T(2,128)S(1)} all-reduce(f32[2,8,2,256]{3,2,1,0:T(2,128)S(1)} %bitcast.92), channel_id=1, replica_groups=mesh['prow'=4,'pcol'=8] {'prow'}, use_global_device_ids=true, to_apply=%region_2.3 | all-reduce | flops 8192 | bytes 65536 | tf_op jit(solution)/shard_map/psum | solution.py:81
  67.8 0.1 fusion.11
  68.0 5.8 %multiply_bitcast_fusion = f32[2,8,1,256,2,1,256]{6,3,4,1,0,5,2:T(8,128)S(1)} fusion(f32[2,8,256,2,256]{4,2,3,1,0:T(8,128)} %copy-done, f32[8,256,2,256]{3,1,2,0:T(8,128)} %broadcast_multiply_fusion, f32[2,8,2,256]{3,2,1,0:T(2,128)S(1)} %copy.14), kind=kLoop, calls=%fused_computation.3 | loop fusion | flops 4194304 | bytes 21004288 | tf_op jit(solution)/shard_map/reshape | solution.py:94
  73.8 9.9 %copy.15 = f32[2,8,1,256,2,1,256]{6,5,4,3,2,1,0:T(1,128)} copy(f32[2,8,1,256,2,1,256]{6,3,4,1,0,5,2:T(8,128)S(1)} %multiply_bitcast_fusion) | data formatting | bytes 16777216 | tf_op jit(solution)/shard_map/reshape | solution.py:94
  (19 shorter events, 0.3 us)
Async XLA Ops:
  3.5 3.4 %copy-start.1 = (f32[2,8,256,2,256]{2,4,3,1,0:T(8,128)}, f32[2,8,256,2,256]{2,4,3,1,0:T(8,128)S(1)}, u32[]{:S(2)}) copy-start(f32[2,8,256,2,256]{2,4,3,1,0:T(8,128)S(1)} %fusion.8) | copy-start | bytes 25165828
  6.9 12.7 %collective-permute-start = (f32[2,8,256,2]{2,3,1,0:T(2,128)S(1)}, f32[2,8,256,2]{2,3,1,0:T(2,128)S(1)}, u32[]{:S(2)}, u32[]{:S(2)}) collective-permute-start(f32[2,8,256,2]{2,3,1,0:T(2,128)S(1)} %bitcast.89), channel_id=1, source_target_pairs={{0,7},{1,0},{2,1},{3,2},{4,3},{5,4},{6,5},{7,6},{8,15},{9,8},{10,9... | collective-permute-start | bytes 98312 | tf_op jit(solution)/shard_map/ppermute | solution.py:60
  13.0 6.6 %collective-permute-start.1 = (f32[2,8,256,2]{2,3,1,0:T(2,128)S(1)}, f32[2,8,256,2]{2,3,1,0:T(2,128)S(1)}, u32[]{:S(2)}, u32[]{:S(2)}) collective-permute-start(f32[2,8,256,2]{2,3,1,0:T(2,128)S(1)} %bitcast.90), channel_id=1, source_target_pairs={{0,1},{1,2},{2,3},{3,4},{4,5},{5,6},{6,7},{7,0},{8,9},{9,10},{10,1... | collective-permute-start | bytes 98312 | tf_op jit(solution)/shard_map/ppermute | solution.py:58
  19.6 6.6 %collective-permute-start.3 = (f32[2,8,256,2]{2,3,1,0:T(2,128)S(1)}, f32[2,8,256,2]{2,3,1,0:T(2,128)S(1)}, u32[]{:S(2)}, u32[]{:S(2)}) collective-permute-start(f32[2,8,256,2]{2,3,1,0:T(2,128)S(1)} %collective-permute-done.1), channel_id=1, source_target_pairs={{0,1},{1,2},{2,3},{3,4},{4,5},{5,6},{6,7},{7,0},{8,9},{9,10},{10,1... | collective-permute-start | bytes 98312 | tf_op jit(solution)/shard_map/ppermute | solution.py:58
  19.6 6.9 %collective-permute-start.2 = (f32[2,8,256,2]{2,3,1,0:T(2,128)S(1)}, f32[2,8,256,2]{2,3,1,0:T(2,128)S(1)}, u32[]{:S(2)}, u32[]{:S(2)}) collective-permute-start(f32[2,8,256,2]{2,3,1,0:T(2,128)S(1)} %collective-permute-done), channel_id=1, source_target_pairs={{0,7},{1,0},{2,1},{3,2},{4,3},{5,4},{6,5},{7,6},{8,15},{9,8},{10,9... | collective-permute-start | bytes 98312 | tf_op jit(solution)/shard_map/ppermute | solution.py:60
  26.2 6.6 %collective-permute-start.5 = (f32[2,8,256,2]{2,3,1,0:T(2,128)S(1)}, f32[2,8,256,2]{2,3,1,0:T(2,128)S(1)}, u32[]{:S(2)}, u32[]{:S(2)}) collective-permute-start(f32[2,8,256,2]{2,3,1,0:T(2,128)S(1)} %collective-permute-done.3), channel_id=1, source_target_pairs={{0,1},{1,2},{2,3},{3,4},{4,5},{5,6},{6,7},{7,0},{8,9},{9,10},{10,1... | collective-permute-start | bytes 98312 | tf_op jit(solution)/shard_map/ppermute | solution.py:58
  26.5 6.6 %collective-permute-start.4 = (f32[2,8,256,2]{2,3,1,0:T(2,128)S(1)}, f32[2,8,256,2]{2,3,1,0:T(2,128)S(1)}, u32[]{:S(2)}, u32[]{:S(2)}) collective-permute-start(f32[2,8,256,2]{2,3,1,0:T(2,128)S(1)} %collective-permute-done.2), channel_id=1, source_target_pairs={{0,7},{1,0},{2,1},{3,2},{4,3},{5,4},{6,5},{7,6},{8,15},{9,8},{10,9... | collective-permute-start | bytes 98312 | tf_op jit(solution)/shard_map/ppermute | solution.py:60
  32.8 6.6 %collective-permute-start.6 = (f32[2,8,256,2]{2,3,1,0:T(2,128)S(1)}, f32[2,8,256,2]{2,3,1,0:T(2,128)S(1)}, u32[]{:S(2)}, u32[]{:S(2)}) collective-permute-start(f32[2,8,256,2]{2,3,1,0:T(2,128)S(1)} %collective-permute-done.5), channel_id=1, source_target_pairs={{0,1},{1,2},{2,3},{3,4},{4,5},{5,6},{6,7},{7,0},{8,9},{9,10},{10,1... | collective-permute-start | bytes 98312 | tf_op jit(solution)/shard_map/ppermute | solution.py:58
  47.0 3.4 %copy-start = (f32[2,8,256,2,256]{4,2,3,1,0:T(8,128)}, f32[2,8,256,2,256]{4,2,3,1,0:T(8,128)S(1)}, u32[]{:S(2)}) copy-start(f32[2,8,256,2,256]{4,2,3,1,0:T(8,128)S(1)} %fusion.5) | copy-start | bytes 25165828
